TPU v7x, 32 devices: a whole 2x2x4 slice. The times are simulated.
32 devices in a mesh: spec: 4 (over y, core), lat: 8 (over z, x).
Axes of the slice: x: 2, y: 2, z: 4, core: 2. Of those that a mesh axis runs over, the one named last changes fastest.
Arguments:
- concentration: float32 [256, 32, 512], P('spec', 'lat'), may hold values from 0.05 to 2
- courant: float32 [32, 512], P('lat'), may hold values from -0.9 to 0.9
- rate_const: float32 [1024], replicated, may hold values from 0.005 to 0.08
- reactants: int32 [1024, 2], replicated, may hold values from 0 to 255
- products: int32 [1024, 2], replicated, may hold values from 0 to 255
- daylit: int32 [32], replicated, may hold values from 0 to 1, as said below
- block_slot: int32 [32], replicated, may hold values from 0 to 31, as said below
Outputs:
- states: float32 [256, 32, 512], P(None, 'lat', 'spec')
Inputs may be any that keep to these rules, and one draw needn't show every extreme that they name: block_slot is a permutation of the 32 rows. Grouping rows into groups of 4 in order, every row's slot lies in its own group or in the group just before or after it, and every group moves exactly one row into each neighbouring group that exists. Of the 4 slots of every group, exactly 2 are taken by rows with daylit equal to 1.
All inputs are finite; a program needn't handle non-finite values.
Results may differ from a plain program's by a relative error of at most 0.0003.
Values sent between devices are 32-bit elements; how exact they have to be, the bound alone decides.
No kernel may reach another device: no remote copies, remote signals or barrier semaphores. Data moves between devices by JAX's collectives and lax.ppermute only.
A program may use at most 64 MiB of HBM per device.

v0:
```python
import jax
import jax.numpy as jnp
from jax import lax
from jax.sharding import PartitionSpec as P

ADV_STEPS = 2
SUBSTEPS = 2


def padded_2(block, sides, width):
    for axis, dim in sides:
        count = lax.axis_size(axis)
        forward = [(i, i + 1) for i in range(count - 1)]
        backward = [(target, source) for source, target in forward]
        low = lax.ppermute(
            lax.slice_in_dim(block, block.shape[dim] - width, None, axis=dim), axis, forward
        )
        high = lax.ppermute(lax.slice_in_dim(block, 0, width, axis=dim), axis, backward)
        block = jnp.concatenate([low, block, high], axis=dim)
    return block


def passed_along(value, axis, by):
    peers = lax.axis_size(axis)
    pairs = [(i, i + by) for i in range(peers) if 0 <= i + by < peers]
    return lax.ppermute(value, axis, pairs)


def minmod(left, right):
    return 0.5 * (jnp.sign(left) + jnp.sign(right)) * jnp.minimum(jnp.abs(left), jnp.abs(right))


def sweep_rows(values, flow_rows, first_row, lat_total):
    row_count = values.shape[1]
    steps_up = values[:, 1:] - values[:, :-1]
    slopes = minmod(steps_up[:, 1:], steps_up[:, :-1])
    face_index = first_row + 2 + jnp.arange(row_count - 3, dtype=jnp.int32)
    inside = ((face_index >= 1) & (face_index <= lat_total - 1))[:, None]
    numbers = jnp.where(inside, flow_rows[2 : row_count - 1], 0.0)
    forward = jnp.maximum(numbers, 0.0) * (
        values[:, 1 : row_count - 2] + 0.5 * (1.0 - numbers) * slopes[:, 0 : row_count - 3]
    )
    backward = jnp.minimum(numbers, 0.0) * (
        values[:, 2 : row_count - 1] - 0.5 * (1.0 + numbers) * slopes[:, 1 : row_count - 2]
    )
    fluxes = forward + backward
    return values[:, 2 : row_count - 2] - (fluxes[:, 1:] - fluxes[:, :-1])


def react_cells(conc, reactants, products, rate_const):
    species_count = conc.shape[0]
    for repeat in range(SUBSTEPS):
        first_conc = jnp.take(conc, reactants[:, 0], axis=0)
        second_conc = jnp.take(conc, reactants[:, 1], axis=0)
        encounter = first_conc * second_conc
        rates = rate_const[:, None] * encounter / (1.0 + jnp.abs(encounter))
        gained = jax.ops.segment_sum(rates, products[:, 0], num_segments=species_count)
        gained = gained + jax.ops.segment_sum(rates, products[:, 1], num_segments=species_count)
        lost = jax.ops.segment_sum(rates, reactants[:, 0], num_segments=species_count)
        lost = lost + jax.ops.segment_sum(rates, reactants[:, 1], num_segments=species_count)
        conc = conc + (gained - lost)
    return conc


def on_device(concentration, courant, rate_const, reactants, products, daylit, block_slot):
    lat_rows = concentration.shape[1]
    lat_index = lax.axis_index("lat")
    lat_total = lat_rows * lax.axis_size("lat")
    base_row = lat_index * lat_rows
    values = concentration
    for repeat in range(ADV_STEPS):
        stacked = jnp.concatenate([values, courant[None]], 0)
        padded = padded_2(stacked, (("lat", 1),), 2)
        values = sweep_rows(padded[:-1], padded[-1], base_row - 2, lat_total)
    cells = lax.all_to_all(values, "spec", split_axis=2, concat_axis=0, tiled=True)
    row_ids = jnp.arange(lat_rows, dtype=jnp.int32)
    my_slots = lax.dynamic_slice_in_dim(block_slot, base_row, lat_rows)
    my_target = my_slots // lat_rows
    received = []
    for direction in (1, -1):
        chosen = jnp.sum(jnp.where(my_target == lat_index + direction, row_ids, 0))
        outgoing = lax.dynamic_index_in_dim(cells, chosen, 1, keepdims=True)
        received.append(passed_along(outgoing, "lat", direction))
    candidates = jnp.concatenate([cells] + received, 1)
    own_slots = base_row + row_ids
    matches = (block_slot[None, :] == own_slots[:, None]).astype(jnp.int32)
    all_rows = jnp.arange(block_slot.shape[0], dtype=jnp.int32)
    source = jnp.sum(matches * all_rows[None, :], axis=1)
    day_flag = jnp.sum(matches * daylit[None, :], axis=1)
    source_band = source // lat_rows
    pick_index = jnp.where(
        source_band == lat_index,
        source - base_row,
        jnp.where(source_band < lat_index, lat_rows, lat_rows + 1),
    )
    gathered = jnp.take(candidates, pick_index, axis=1)
    species_count = gathered.shape[0]
    day_count = lat_rows // 2
    ranking = jnp.cumsum(day_flag) - 1
    wanted = (day_flag[None, :] == 1) & (
        ranking[None, :] == jnp.arange(day_count, dtype=jnp.int32)[:, None]
    )
    lit_slots = jnp.sum(wanted.astype(jnp.int32) * row_ids[None, :], axis=1)
    active = jnp.take(gathered, lit_slots, axis=1)
    reacted = react_cells(
        active.reshape(species_count, -1), reactants, products, rate_const
    ).reshape(active.shape)
    states = gathered.at[:, lit_slots].set(reacted)
    return states


def solution(mesh):
    in_specs = (P("spec", "lat", None), P("lat", None), P(), P(), P(), P(), P())
    out_specs = P(None, "lat", "spec")
    return jax.shard_map(
        on_device, mesh=mesh, in_specs=in_specs, out_specs=out_specs, check_vma=False
    )
```

profile of v0, /device:TPU:0, one launch (start us, length us, event | category | flops | bytes accessed | tf_op | source)
XLA Modules:
  0.0 146.5 jit_solution(2726070398159518174)
XLA Ops:
  0.0 1.6 %pad_maximum_fusion.8 = (f32[65,2,512]{2,1,0:T(2,128)S(1)}, f32[65,2,512]{2,1,0:T(2,128)S(1)}) fusion(f32[1,4,512]{2,1,0:T(4,128)} %bitcast.71, f32[64,4,512]{2,1,0:T(4,128)} %param.9), kind=kLoop, calls=%fused_computation.61 | loop fusion | flops 133120 | bytes 1064960 | tf_op jit(solution)/shard_map/concatenate | solution.py:72
  1.7 1.4 collective-permute-start
  3.2 5.5 %collective-permute-start.1 = (f32[65,2,512]{2,0,1:T(8,128)S(1)}, f32[65,2,512]{2,0,1:T(8,128)S(1)}, u32[]{:S(2)}, u32[]{:S(2)}) collective-permute-start(f32[65,2,512]{2,0,1:T(8,128)S(1)} %copy.68), channel_id=1, source_target_pairs={{0,1},{1,2},{2,3},{3,4},{4,5},{5,6},{6,7},{8,9},{9,10},{10,11},{11... | collective-permute-start | bytes 798728 | tf_op jit(solution)/shard_map/ppermute | solution.py:15
  9.4 4.3 %collective-permute-done = f32[65,2,512]{2,0,1:T(8,128)S(1)} collective-permute-done((f32[65,2,512]{2,0,1:T(8,128)S(1)}, f32[65,2,512]{2,0,1:T(8,128)S(1)}, u32[]{:S(2)}, u32[]{:S(2)}) %collective-permute-start) | collective-permute-done | bytes 266272 | tf_op jit(solution)/shard_map/ppermute | solution.py:18
  14.2 6.0 %collective-permute-done.1 = f32[65,2,512]{2,0,1:T(8,128)S(1)} collective-permute-done((f32[65,2,512]{2,0,1:T(8,128)S(1)}, f32[65,2,512]{2,0,1:T(8,128)S(1)}, u32[]{:S(2)}, u32[]{:S(2)}) %collective-permute-start.1) | collective-permute-done | bytes 266272 | tf_op jit(solution)/shard_map/ppermute | solution.py:15
  22.8 1.3 collective-permute-start.2
  24.1 0.8 fusion.43
  29.0 5.0 %collective-permute-start.3 = (f32[65,2,512]{2,0,1:T(8,128)S(1)}, f32[65,2,512]{2,0,1:T(8,128)S(1)}, u32[]{:S(2)}, u32[]{:S(2)}) collective-permute-start(f32[65,2,512]{2,0,1:T(8,128)S(1)} %copy.74), channel_id=1, source_target_pairs={{0,1},{1,2},{2,3},{3,4},{4,5},{5,6},{6,7},{8,9},{9,10},{10,11},{11... | collective-permute-start | bytes 798728 | tf_op jit(solution)/shard_map/ppermute | solution.py:15
  34.8 6.0 %collective-permute-done.3 = f32[65,2,512]{2,0,1:T(8,128)S(1)} collective-permute-done((f32[65,2,512]{2,0,1:T(8,128)S(1)}, f32[65,2,512]{2,0,1:T(8,128)S(1)}, u32[]{:S(2)}, u32[]{:S(2)}) %collective-permute-start.3) | collective-permute-done | bytes 266272 | tf_op jit(solution)/shard_map/ppermute | solution.py:15
  43.6 1.8 %reshape.360 = f32[4,1,32768]{2,1,0:T(1,128)} reshape(f32[512,4,64]{2,1,0:T(4,128)S(1)} %bitcast.65) | data formatting | bytes 1048576
  45.4 3.5 %all-to-all-start = ((f32[4,1,32768]{2,1,0:T(1,128)}), f32[4,1,32768]{2,1,0:T(1,128)S(1)}, u32[]{:S(2)}, u32[]{:S(2)}) async-start(f32[4,1,32768]{2,1,0:T(1,128)} %reshape.360), calls=%async_computation | async-start | bytes 1048576 | tf_op jit(solution)/shard_map/all_to_all | solution.py:75
  49.0 8.7 %all-to-all-done = f32[4,1,32768]{2,1,0:T(1,128)S(1)} async-done(((f32[4,1,32768]{2,1,0:T(1,128)}), f32[4,1,32768]{2,1,0:T(1,128)S(1)}, u32[]{:S(2)}, u32[]{:S(2)}) %all-to-all-start) | async-done | bytes 524320 | tf_op jit(solution)/shard_map/all_to_all | solution.py:75
  58.2 2.1 %reduce = f32[4,32768]{1,0:T(4,128)S(1)} reduce(f32[4,1,32768]{2,1,0:T(1,128)S(1)} %all-to-all-done, f32[]{:T(128)} %broadcast.400), dimensions={1}, to_apply=%all_to_all.13.reduce_sub_computation | reduce | bytes 1048580 | tf_op jit(solution)/shard_map/all_to_all | solution.py:75
  61.4 1.3 collective-permute-start.5
  62.7 5.2 %collective-permute-start.4 = (f32[256,1,128]{2,0,1:T(8,128)S(1)}, f32[256,1,128]{2,0,1:T(8,128)S(1)}, u32[]{:S(2)}, u32[]{:S(2)}) collective-permute-start(f32[256,1,128]{2,0,1:T(8,128)S(1)} %get-tuple-element.22), channel_id=1, source_target_pairs={{0,1},{1,2},{2,3},{3,4},{4,5},{5,6},{6,7},{8,9},{9,10},{10,11},{11... | collective-permute-start | bytes 393224 | tf_op jit(solution)/shard_map/ppermute | solution.py:26
  68.0 1.0 collective-permute-done.5
  69.0 3.5 %collective-permute-done.4 = f32[256,1,128]{2,0,1:T(8,128)S(1)} collective-permute-done((f32[256,1,128]{2,0,1:T(8,128)S(1)}, f32[256,1,128]{2,0,1:T(8,128)S(1)}, u32[]{:S(2)}, u32[]{:S(2)}) %collective-permute-start.4) | collective-permute-done | bytes 131104 | tf_op jit(solution)/shard_map/ppermute | solution.py:26
  74.1 3.5 %gather_fusion.3 = f32[1024,256]{1,0:T(8,128)S(1)} fusion(f32[256,256]{1,0:T(8,128)S(1)} %broadcast_select_fusion, s32[1024]{0:T(1024)S(1)} %fusion.39), kind=kCustom, calls=%fused_computation.1.clone | custom fusion | bytes 2101248 | tf_op jit(solution)/shard_map/jit(_take)/gather | solution.py:54
  77.6 3.5 %gather_fusion.2 = f32[1024,256]{1,0:T(8,128)S(1)} fusion(f32[256,256]{1,0:T(8,128)S(1)} %broadcast_select_fusion, s32[1024]{0:T(1024)S(1)} %fusion.38), kind=kCustom, calls=%fused_computation.clone | custom fusion | bytes 2101248 | tf_op jit(solution)/shard_map/jit(_take)/gather | solution.py:53
  81.1 1.7 %add_divide_fusion.1 = f32[1024,256]{1,0:T(8,128)} fusion(f32[1024,256]{1,0:T(8,128)S(1)} %gather_fusion.3, f32[1024,256]{1,0:T(8,128)S(1)} %gather_fusion.2, f32[1024]{0:T(1024)S(1)} %copy-done.2, pred[1024]{0:T(1024)(128)(4,1)S(1)} %get-tuple-element.28, pred[1024]{0:T(1024)(128)(4,1)S(1)} %get-tuple-element.29), kind=kLoop, calls=%fused_computation.48 | loop fusion | flops 1835008 | bytes 3151872 | tf_op jit(solution)/shard_map/div | solution.py:56
  82.8 6.6 %scatter_custom_fusion.2 = f32[256,256]{1,0:T(8,128)S(1)} fusion(s32[1024]{0:T(1024)S(1)} %bitcast.85, f32[1024,256]{1,0:T(8,128)} %add_divide_fusion.1, f32[]{:T(128)} %constant.99.clone.1), kind=kCustom, calls=%fused_computation.77 | custom fusion | flops 262144 | bytes 262656 | tf_op jit(solution)/shard_map/scatter-add | solution.py:59
  89.4 6.6 %scatter_custom_fusion.3 = f32[256,256]{1,0:T(8,128)S(1)} fusion(s32[1024]{0:T(1024)S(1)} %bitcast.81, f32[1024,256]{1,0:T(8,128)} %add_divide_fusion.1, f32[]{:T(128)} %constant.99.clone.1), kind=kCustom, calls=%fused_computation.75 | custom fusion | flops 262144 | bytes 262656 | tf_op jit(solution)/shard_map/scatter-add | solution.py:60
  96.0 6.6 %scatter_custom_fusion = f32[256,256]{1,0:T(8,128)S(1)} fusion(s32[1024]{0:T(1024)S(1)} %bitcast.89, f32[1024,256]{1,0:T(8,128)} %add_divide_fusion.1, f32[]{:T(128)} %constant.99.clone.1), kind=kCustom, calls=%fused_computation.81 | custom fusion | flops 262144 | bytes 262656 | tf_op jit(solution)/shard_map/scatter-add | solution.py:57
  102.6 6.8 %scatter_custom_fusion.1 = f32[256,256]{1,0:T(8,128)S(1)} fusion(s32[1024]{0:T(1024)S(1)} %bitcast.87, f32[1024,256]{1,0:T(8,128)} %add_divide_fusion.1, f32[]{:T(128)} %constant.99.clone.1), kind=kCustom, calls=%fused_computation.79 | custom fusion | flops 262144 | bytes 262656 | tf_op jit(solution)/shard_map/scatter-add | solution.py:58
  109.5 3.5 %gather_fusion.5 = f32[1024,256]{1,0:T(8,128)S(1)} fusion(f32[256,256]{1,0:T(8,128)S(1)} %subtract_add_fusion, s32[1024]{0:T(1024)S(1)} %fusion.39), kind=kCustom, calls=%fused_computation.3.clone | custom fusion | bytes 2101248 | tf_op jit(solution)/shard_map/jit(_take)/gather | solution.py:54
  113.0 3.5 %gather_fusion.4 = f32[1024,256]{1,0:T(8,128)S(1)} fusion(f32[256,256]{1,0:T(8,128)S(1)} %subtract_add_fusion, s32[1024]{0:T(1024)S(1)} %fusion.38), kind=kCustom, calls=%fused_computation.2.clone | custom fusion | bytes 2101248 | tf_op jit(solution)/shard_map/jit(_take)/gather | solution.py:53
  116.5 1.7 %add_divide_fusion = f32[1024,256]{1,0:T(8,128)} fusion(f32[1024,256]{1,0:T(8,128)S(1)} %gather_fusion.5, f32[1024,256]{1,0:T(8,128)S(1)} %gather_fusion.4, f32[1024]{0:T(1024)S(1)} %copy-done.2, pred[1024]{0:T(1024)(128)(4,1)S(1)} %get-tuple-element.28, pred[1024]{0:T(1024)(128)(4,1)S(1)} %get-tuple-element.29), kind=kLoop, calls=%fused_computation.47 | loop fusion | flops 1835008 | bytes 3151872 | tf_op jit(solution)/shard_map/div | solution.py:56
  118.2 6.6 %scatter_custom_fusion.6 = f32[256,256]{1,0:T(8,128)S(1)} fusion(s32[1024]{0:T(1024)S(1)} %bitcast.86, f32[1024,256]{1,0:T(8,128)} %add_divide_fusion, f32[]{:T(128)} %constant.99.clone.1), kind=kCustom, calls=%fused_computation.69 | custom fusion | flops 262144 | bytes 262656 | tf_op jit(solution)/shard_map/scatter-add | solution.py:59
  124.8 6.6 %scatter_custom_fusion.7 = f32[256,256]{1,0:T(8,128)S(1)} fusion(s32[1024]{0:T(1024)S(1)} %bitcast.82, f32[1024,256]{1,0:T(8,128)} %add_divide_fusion, f32[]{:T(128)} %constant.99.clone.1), kind=kCustom, calls=%fused_computation.67 | custom fusion | flops 262144 | bytes 262656 | tf_op jit(solution)/shard_map/scatter-add | solution.py:60
  131.4 6.6 %scatter_custom_fusion.4 = f32[256,256]{1,0:T(8,128)S(1)} fusion(s32[1024]{0:T(1024)S(1)} %bitcast.90, f32[1024,256]{1,0:T(8,128)} %add_divide_fusion, f32[]{:T(128)} %constant.99.clone.1), kind=kCustom, calls=%fused_computation.73 | custom fusion | flops 262144 | bytes 262656 | tf_op jit(solution)/shard_map/scatter-add | solution.py:57
  138.0 6.6 %scatter_custom_fusion.5 = f32[256,256]{1,0:T(8,128)S(1)} fusion(s32[1024]{0:T(1024)S(1)} %bitcast.88, f32[1024,256]{1,0:T(8,128)} %add_divide_fusion, f32[]{:T(128)} %constant.99.clone.1), kind=kCustom, calls=%fused_computation.71 | custom fusion | flops 262144 | bytes 262656 | tf_op jit(solution)/shard_map/scatter-add | solution.py:58
  145.3 1.1 copy.84
  (72 shorter events, 11.4 us)
Async XLA Ops:
  0.0 8.7 %copy-start.5 = (s32[32]{0:T(128)S(1)}, s32[32]{0:T(128)}, u32[]{:S(2)}) copy-start(s32[32]{0:T(128)} %param.15) | copy-start | bytes 388
  0.0 8.7 %copy-start.6 = (s32[32]{0:T(128)S(1)}, s32[32]{0:T(128)}, u32[]{:S(2)}) copy-start(s32[32]{0:T(128)} %param.14) | copy-start | bytes 388
  0.0 9.0 %copy-start.3 = (s32[1024,2]{0,1:T(2,128)S(1)}, s32[1024,2]{0,1:T(2,128)}, u32[]{:S(2)}) copy-start(s32[1024,2]{0,1:T(2,128)} %param.12) | copy-start | bytes 24580
  1.6 12.3 %copy-start = (f32[64,4,512]{2,1,0:T(4,128)S(1)}, f32[64,4,512]{2,1,0:T(4,128)}, u32[]{:S(2)}) copy-start(f32[64,4,512]{2,1,0:T(4,128)} %param.9) | copy-start | bytes 1572868
  1.6 12.3 %copy-start.1 = (f32[4,512]{1,0:T(4,128)S(1)}, f32[4,512]{1,0:T(4,128)}, u32[]{:S(2)}) copy-start(f32[4,512]{1,0:T(4,128)} %param.10) | copy-start | bytes 24580
  1.7 12.0 %collective-permute-start = (f32[65,2,512]{2,0,1:T(8,128)S(1)}, f32[65,2,512]{2,0,1:T(8,128)S(1)}, u32[]{:S(2)}, u32[]{:S(2)}) collective-permute-start(f32[65,2,512]{2,0,1:T(8,128)S(1)} %copy.66), channel_id=1, source_target_pairs={{1,0},{2,1},{3,2},{4,3},{5,4},{6,5},{7,6},{9,8},{10,9},{11,10},{12... | collective-permute-start | bytes 798728 | tf_op jit(solution)/shard_map/ppermute | solution.py:18
  3.2 17.0 %collective-permute-start.1 = (f32[65,2,512]{2,0,1:T(8,128)S(1)}, f32[65,2,512]{2,0,1:T(8,128)S(1)}, u32[]{:S(2)}, u32[]{:S(2)}) collective-permute-start(f32[65,2,512]{2,0,1:T(8,128)S(1)} %copy.68), channel_id=1, source_target_pairs={{0,1},{1,2},{2,3},{3,4},{4,5},{5,6},{6,7},{8,9},{9,10},{10,11},{11... | collective-permute-start | bytes 798728 | tf_op jit(solution)/shard_map/ppermute | solution.py:15
  22.8 11.6 %collective-permute-start.2 = (f32[65,2,512]{2,0,1:T(8,128)S(1)}, f32[65,2,512]{2,0,1:T(8,128)S(1)}, u32[]{:S(2)}, u32[]{:S(2)}) collective-permute-start(f32[65,2,512]{2,0,1:T(8,128)S(1)} %copy.72), channel_id=1, source_target_pairs={{1,0},{2,1},{3,2},{4,3},{5,4},{6,5},{7,6},{9,8},{10,9},{11,10},{12... | collective-permute-start | bytes 798728 | tf_op jit(solution)/shard_map/ppermute | solution.py:18
  29.0 11.9 %collective-permute-start.3 = (f32[65,2,512]{2,0,1:T(8,128)S(1)}, f32[65,2,512]{2,0,1:T(8,128)S(1)}, u32[]{:S(2)}, u32[]{:S(2)}) collective-permute-start(f32[65,2,512]{2,0,1:T(8,128)S(1)} %copy.74), channel_id=1, source_target_pairs={{0,1},{1,2},{2,3},{3,4},{4,5},{5,6},{6,7},{8,9},{9,10},{10,11},{11... | collective-permute-start | bytes 798728 | tf_op jit(solution)/shard_map/ppermute | solution.py:15
  43.6 5.3 %copy-start.4 = (s32[1024,2]{0,1:T(2,128)S(1)}, s32[1024,2]{0,1:T(2,128)}, u32[]{:S(2)}) copy-start(s32[1024,2]{0,1:T(2,128)} %param.13) | copy-start | bytes 24580
  45.4 12.3 %all-to-all-start = ((f32[4,1,32768]{2,1,0:T(1,128)}), f32[4,1,32768]{2,1,0:T(1,128)S(1)}, u32[]{:S(2)}, u32[]{:S(2)}) async-start(f32[4,1,32768]{2,1,0:T(1,128)} %reshape.360), calls=%async_computation | async-start | bytes 1048576 | tf_op jit(solution)/shard_map/all_to_all | solution.py:75
  61.4 7.6 %collective-permute-start.5 = (f32[256,1,128]{2,0,1:T(8,128)S(1)}, f32[256,1,128]{2,0,1:T(8,128)S(1)}, u32[]{:S(2)}, u32[]{:S(2)}) collective-permute-start(f32[256,1,128]{2,0,1:T(8,128)S(1)} %get-tuple-element.23), channel_id=1, source_target_pairs={{1,0},{2,1},{3,2},{4,3},{5,4},{6,5},{7,6},{9,8},{10,9},{11,10},{12... | collective-permute-start | bytes 393224 | tf_op jit(solution)/shard_map/ppermute | solution.py:26
  62.7 9.7 %collective-permute-start.4 = (f32[256,1,128]{2,0,1:T(8,128)S(1)}, f32[256,1,128]{2,0,1:T(8,128)S(1)}, u32[]{:S(2)}, u32[]{:S(2)}) collective-permute-start(f32[256,1,128]{2,0,1:T(8,128)S(1)} %get-tuple-element.22), channel_id=1, source_target_pairs={{0,1},{1,2},{2,3},{3,4},{4,5},{5,6},{6,7},{8,9},{9,10},{10,11},{11... | collective-permute-start | bytes 393224 | tf_op jit(solution)/shard_map/ppermute | solution.py:26
  77.6 3.5 %copy-start.2 = (f32[1024]{0:T(1024)S(1)}, f32[1024]{0:T(1024)}, u32[]{:S(2)}) copy-start(f32[1024]{0:T(1024)} %param.11) | copy-start | bytes 12292
where the time goes:
time: 147 us; the launch traced here: 146 us
  other arithmetic  66.8 us (45%)
  waiting for transfers between devices  29.9 us (20%)
  starting transfers between devices  23.2 us (16%)
  local copies, waits for them, and re-layouts  22 us (15%)
  between operations  4.58 us (3%)
    scatter-add x2, other arithmetic, react_cells(): jax.ops.segment_sum(rates, products[:, 1], num_segments=species_count)  13.4 us
    scatter-add x2, other arithmetic, react_cells(): jax.ops.segment_sum(rates, reactants[:, 1], num_segments=species_count)  13.2 us
    scatter-add x2, other arithmetic, react_cells(): jax.ops.segment_sum(rates, products[:, 0], num_segments=species_count)  13.2 us
    scatter-add x2, other arithmetic, react_cells(): jax.ops.segment_sum(rates, reactants[:, 0], num_segments=species_count)  13.2 us
    ppermute x2, waiting for transfers between devices, padded_2(): lax.ppermute(lax.slice_in_dim(block, block.shape[dim] - width, None, axis...  12.1 us
    ppermute x2, starting transfers between devices, padded_2(): lax.ppermute(lax.slice_in_dim(block, block.shape[dim] - width, None, axis...  10.6 us
    all_to_all x1, waiting for transfers between devices, on_device(): lax.all_to_all(values, 'spec', split_axis=2, concat_axis=0, tiled=True)  8.69 us
    gather x2, local copies, waits for them, and re-layouts, react_cells(): first_conc = jnp.take(conc, reactants[:, 0], axis=0)  6.93 us
  transfers between devices with their start and end apart: 7, of which 7 were waited for; matrix products, arithmetic and copies ran while one was open for 2% of the time, Pallas kernels for 0%

commit v1 on v0

--- a/solution.py
+++ b/solution.py
@@ -72,7 +72,11 @@
         stacked = jnp.concatenate([values, courant[None]], 0)
         padded = padded_2(stacked, (("lat", 1),), 2)
         values = sweep_rows(padded[:-1], padded[-1], base_row - 2, lat_total)
-    cells = lax.all_to_all(values, "spec", split_axis=2, concat_axis=0, tiled=True)
+    build_terms = lambda sheet: jnp.concatenate(
+        lax.all_to_all(jnp.stack(jnp.split(sheet, lax.axis_size("spec"), axis=2)), "spec", 0, 0),
+        axis=0,
+    )
+    cells = build_terms(values)
     row_ids = jnp.arange(lat_rows, dtype=jnp.int32)
     my_slots = lax.dynamic_slice_in_dim(block_slot, base_row, lat_rows)
     my_target = my_slots // lat_rows

time: 147 us -> 142 us (0.966)
  local copies, waits for them, and re-layouts: 22 us -> 18.4 us
    unnamed x16 -> x14, local copies, waits for them, and re-layouts: 2.52 us -> 0.04 us
    all_to_all x1 -> x0, other arithmetic: 2.14 us -> none  [on_device(): lax.all_to_all(values, 'spec', split_axis=2, concat_axis=0, tiled=True)]
where the time goes in v1:
time: 142 us
  other arithmetic  65.7 us (46%)
  waiting for transfers between devices  30.1 us (21%)
  starting transfers between devices  23.1 us (16%)
  local copies, waits for them, and re-layouts  18.4 us (13%)
  between operations  4.57 us (3%)
    scatter-add x2, other arithmetic, react_cells(): jax.ops.segment_sum(rates, reactants[:, 0], num_segments=species_count)  13.6 us
    scatter-add x2, other arithmetic, react_cells(): jax.ops.segment_sum(rates, reactants[:, 1], num_segments=species_count)  13.2 us
    scatter-add x2, other arithmetic, react_cells(): jax.ops.segment_sum(rates, products[:, 0], num_segments=species_count)  13.2 us
    scatter-add x2, other arithmetic, react_cells(): jax.ops.segment_sum(rates, products[:, 1], num_segments=species_count)  13.2 us
    ppermute x2, waiting for transfers between devices, padded_2(): lax.ppermute(lax.slice_in_dim(block, block.shape[dim] - width, None, axis...  12.1 us
    ppermute x2, starting transfers between devices, padded_2(): lax.ppermute(lax.slice_in_dim(block, block.shape[dim] - width, None, axis...  10.6 us
    all_to_all x1, waiting for transfers between devices, on_device(): lax.all_to_all(jnp.stack(jnp.split(sheet, lax.axis_size('spec'), axis=2))...  8.69 us
    gather x2, local copies, waits for them, and re-layouts, react_cells(): second_conc = jnp.take(conc, reactants[:, 1], axis=0)  6.93 us
  transfers between devices with their start and end apart: 7, of which 7 were waited for; matrix products, arithmetic and copies ran while one was open for 2% of the time, Pallas kernels for 0%

profile of v1, /device:TPU:0, one launch (start us, length us, event | category | flops | bytes accessed | tf_op | source)
XLA Modules:
  0.0 141.8 jit_solution(613984095993490954)
XLA Ops:
  0.0 1.6 %pad_maximum_fusion.9 = (f32[65,2,512]{2,1,0:T(2,128)S(1)}, f32[65,2,512]{2,1,0:T(2,128)S(1)}) fusion(f32[1,4,512]{2,1,0:T(4,128)} %bitcast.71, f32[64,4,512]{2,1,0:T(4,128)} %param.9), kind=kLoop, calls=%fused_computation.62 | loop fusion | flops 133120 | bytes 1064960 | tf_op jit(solution)/shard_map/concatenate | solution.py:72
  1.7 1.4 %collective-permute-start = (f32[65,2,512]{2,0,1:T(8,128)S(1)}, f32[65,2,512]{2,0,1:T(8,128)S(1)}, u32[]{:S(2)}, u32[]{:S(2)}) collective-permute-start(f32[65,2,512]{2,0,1:T(8,128)S(1)} %copy.43), channel_id=1, source_target_pairs={{1,0},{2,1},{3,2},{4,3},{5,4},{6,5},{7,6},{9,8},{10,9},{11,10},{12... | collective-permute-start | bytes 798728 | tf_op jit(solution)/shard_map/ppermute | solution.py:18
  3.2 5.5 %collective-permute-start.1 = (f32[65,2,512]{2,0,1:T(8,128)S(1)}, f32[65,2,512]{2,0,1:T(8,128)S(1)}, u32[]{:S(2)}, u32[]{:S(2)}) collective-permute-start(f32[65,2,512]{2,0,1:T(8,128)S(1)} %copy.45), channel_id=1, source_target_pairs={{0,1},{1,2},{2,3},{3,4},{4,5},{5,6},{6,7},{8,9},{9,10},{10,11},{11... | collective-permute-start | bytes 798728 | tf_op jit(solution)/shard_map/ppermute | solution.py:15
  9.4 4.3 %collective-permute-done = f32[65,2,512]{2,0,1:T(8,128)S(1)} collective-permute-done((f32[65,2,512]{2,0,1:T(8,128)S(1)}, f32[65,2,512]{2,0,1:T(8,128)S(1)}, u32[]{:S(2)}, u32[]{:S(2)}) %collective-permute-start) | collective-permute-done | bytes 266272 | tf_op jit(solution)/shard_map/ppermute | solution.py:18
  14.2 6.0 %collective-permute-done.1 = f32[65,2,512]{2,0,1:T(8,128)S(1)} collective-permute-done((f32[65,2,512]{2,0,1:T(8,128)S(1)}, f32[65,2,512]{2,0,1:T(8,128)S(1)}, u32[]{:S(2)}, u32[]{:S(2)}) %collective-permute-start.1) | collective-permute-done | bytes 266272 | tf_op jit(solution)/shard_map/ppermute | solution.py:15
  22.8 1.3 collective-permute-start.2
  24.1 0.8 fusion.43
  29.0 5.0 %collective-permute-start.3 = (f32[65,2,512]{2,0,1:T(8,128)S(1)}, f32[65,2,512]{2,0,1:T(8,128)S(1)}, u32[]{:S(2)}, u32[]{:S(2)}) collective-permute-start(f32[65,2,512]{2,0,1:T(8,128)S(1)} %copy.51), channel_id=1, source_target_pairs={{0,1},{1,2},{2,3},{3,4},{4,5},{5,6},{6,7},{8,9},{9,10},{10,11},{11... | collective-permute-start | bytes 798728 | tf_op jit(solution)/shard_map/ppermute | solution.py:15
  34.8 6.0 %collective-permute-done.3 = f32[65,2,512]{2,0,1:T(8,128)S(1)} collective-permute-done((f32[65,2,512]{2,0,1:T(8,128)S(1)}, f32[65,2,512]{2,0,1:T(8,128)S(1)}, u32[]{:S(2)}, u32[]{:S(2)}) %collective-permute-start.3) | collective-permute-done | bytes 266272 | tf_op jit(solution)/shard_map/ppermute | solution.py:15
  41.6 0.7 minimum_multiply_fusion
  43.3 0.9 pad_maximum_fusion.7
  44.2 3.5 %all-to-all-start = ((f32[4,64,4,128]{3,2,1,0:T(4,128)}), f32[4,64,4,128]{3,2,1,0:T(4,128)S(1)}, u32[]{:S(2)}, u32[]{:S(2)}) async-start(f32[4,64,4,128]{3,2,1,0:T(4,128)} %pad_maximum_fusion.7), calls=%async_computation | async-start | bytes 1048576 | tf_op jit(solution)/shard_map/all_to_all | solution.py:76
  47.8 8.7 %all-to-all-done = f32[4,64,4,128]{3,2,1,0:T(4,128)S(1)} async-done(((f32[4,64,4,128]{3,2,1,0:T(4,128)}), f32[4,64,4,128]{3,2,1,0:T(4,128)S(1)}, u32[]{:S(2)}, u32[]{:S(2)}) %all-to-all-start) | async-done | bytes 524320 | tf_op jit(solution)/shard_map/all_to_all | solution.py:76
  56.6 1.3 collective-permute-start.5
  57.9 5.0 %collective-permute-start.4 = (f32[256,1,128]{2,0,1:T(8,128)S(1)}, f32[256,1,128]{2,0,1:T(8,128)S(1)}, u32[]{:S(2)}, u32[]{:S(2)}) collective-permute-start(f32[256,1,128]{2,0,1:T(8,128)S(1)} %get-tuple-element.22), channel_id=1, source_target_pairs={{0,1},{1,2},{2,3},{3,4},{4,5},{5,6},{6,7},{8,9},{9,10},{10,11},{11... | collective-permute-start | bytes 393224 | tf_op jit(solution)/shard_map/ppermute | solution.py:26
  62.9 1.2 collective-permute-done.5
  64.2 3.5 %collective-permute-done.4 = f32[256,1,128]{2,0,1:T(8,128)S(1)} collective-permute-done((f32[256,1,128]{2,0,1:T(8,128)S(1)}, f32[256,1,128]{2,0,1:T(8,128)S(1)}, u32[]{:S(2)}, u32[]{:S(2)}) %collective-permute-start.4) | collective-permute-done | bytes 131104 | tf_op jit(solution)/shard_map/ppermute | solution.py:26
  69.3 3.5 %gather_fusion.3 = f32[1024,256]{1,0:T(8,128)S(1)} fusion(f32[256,256]{1,0:T(8,128)S(1)} %broadcast_select_fusion, s32[1024]{0:T(1024)S(1)} %fusion.39), kind=kCustom, calls=%fused_computation.1.clone | custom fusion | bytes 2101248 | tf_op jit(solution)/shard_map/jit(_take)/gather | solution.py:54
  72.7 3.5 %gather_fusion.2 = f32[1024,256]{1,0:T(8,128)S(1)} fusion(f32[256,256]{1,0:T(8,128)S(1)} %broadcast_select_fusion, s32[1024]{0:T(1024)S(1)} %fusion.38), kind=kCustom, calls=%fused_computation.clone | custom fusion | bytes 2101248 | tf_op jit(solution)/shard_map/jit(_take)/gather | solution.py:53
  76.2 1.7 %add_divide_fusion.1 = f32[1024,256]{1,0:T(8,128)} fusion(f32[1024,256]{1,0:T(8,128)S(1)} %gather_fusion.3, f32[1024,256]{1,0:T(8,128)S(1)} %gather_fusion.2, f32[1024]{0:T(1024)S(1)} %copy-done.2, pred[1024]{0:T(1024)(128)(4,1)S(1)} %get-tuple-element.32, pred[1024]{0:T(1024)(128)(4,1)S(1)} %get-tuple-element.33), kind=kLoop, calls=%fused_computation.48 | loop fusion | flops 1835008 | bytes 3151872 | tf_op jit(solution)/shard_map/div | solution.py:56
  77.9 6.8 %scatter_custom_fusion.2 = f32[256,256]{1,0:T(8,128)S(1)} fusion(s32[1024]{0:T(1024)S(1)} %bitcast.85, f32[1024,256]{1,0:T(8,128)} %add_divide_fusion.1, f32[]{:T(128)} %constant.99.clone.1), kind=kCustom, calls=%fused_computation.82 | custom fusion | flops 262144 | bytes 262656 | tf_op jit(solution)/shard_map/scatter-add | solution.py:59
  84.7 6.6 %scatter_custom_fusion.3 = f32[256,256]{1,0:T(8,128)S(1)} fusion(s32[1024]{0:T(1024)S(1)} %bitcast.81, f32[1024,256]{1,0:T(8,128)} %add_divide_fusion.1, f32[]{:T(128)} %constant.99.clone.1), kind=kCustom, calls=%fused_computation.80 | custom fusion | flops 262144 | bytes 262656 | tf_op jit(solution)/shard_map/scatter-add | solution.py:60
  91.3 6.6 %scatter_custom_fusion = f32[256,256]{1,0:T(8,128)S(1)} fusion(s32[1024]{0:T(1024)S(1)} %bitcast.89, f32[1024,256]{1,0:T(8,128)} %add_divide_fusion.1, f32[]{:T(128)} %constant.99.clone.1), kind=kCustom, calls=%fused_computation.86 | custom fusion | flops 262144 | bytes 262656 | tf_op jit(solution)/shard_map/scatter-add | solution.py:57
  97.9 6.6 %scatter_custom_fusion.1 = f32[256,256]{1,0:T(8,128)S(1)} fusion(s32[1024]{0:T(1024)S(1)} %bitcast.87, f32[1024,256]{1,0:T(8,128)} %add_divide_fusion.1, f32[]{:T(128)} %constant.99.clone.1), kind=kCustom, calls=%fused_computation.84 | custom fusion | flops 262144 | bytes 262656 | tf_op jit(solution)/shard_map/scatter-add | solution.py:58
  104.6 3.5 %gather_fusion.5 = f32[1024,256]{1,0:T(8,128)S(1)} fusion(f32[256,256]{1,0:T(8,128)S(1)} %subtract_add_fusion, s32[1024]{0:T(1024)S(1)} %fusion.39), kind=kCustom, calls=%fused_computation.3.clone | custom fusion | bytes 2101248 | tf_op jit(solution)/shard_map/jit(_take)/gather | solution.py:54
  108.1 3.5 %gather_fusion.4 = f32[1024,256]{1,0:T(8,128)S(1)} fusion(f32[256,256]{1,0:T(8,128)S(1)} %subtract_add_fusion, s32[1024]{0:T(1024)S(1)} %fusion.38), kind=kCustom, calls=%fused_computation.2.clone | custom fusion | bytes 2101248 | tf_op jit(solution)/shard_map/jit(_take)/gather | solution.py:53
  111.6 1.7 %add_divide_fusion = f32[1024,256]{1,0:T(8,128)} fusion(f32[1024,256]{1,0:T(8,128)S(1)} %gather_fusion.5, f32[1024,256]{1,0:T(8,128)S(1)} %gather_fusion.4, f32[1024]{0:T(1024)S(1)} %copy-done.2, pred[1024]{0:T(1024)(128)(4,1)S(1)} %get-tuple-element.32, pred[1024]{0:T(1024)(128)(4,1)S(1)} %get-tuple-element.33), kind=kLoop, calls=%fused_computation.47 | loop fusion | flops 1835008 | bytes 3151872 | tf_op jit(solution)/shard_map/div | solution.py:56
  113.3 6.8 %scatter_custom_fusion.6 = f32[256,256]{1,0:T(8,128)S(1)} fusion(s32[1024]{0:T(1024)S(1)} %bitcast.86, f32[1024,256]{1,0:T(8,128)} %add_divide_fusion, f32[]{:T(128)} %constant.99.clone.1), kind=kCustom, calls=%fused_computation.74 | custom fusion | flops 262144 | bytes 262656 | tf_op jit(solution)/shard_map/scatter-add | solution.py:59
  120.1 6.6 %scatter_custom_fusion.7 = f32[256,256]{1,0:T(8,128)S(1)} fusion(s32[1024]{0:T(1024)S(1)} %bitcast.82, f32[1024,256]{1,0:T(8,128)} %add_divide_fusion, f32[]{:T(128)} %constant.99.clone.1), kind=kCustom, calls=%fused_computation.72 | custom fusion | flops 262144 | bytes 262656 | tf_op jit(solution)/shard_map/scatter-add | solution.py:60
  126.7 6.6 %scatter_custom_fusion.4 = f32[256,256]{1,0:T(8,128)S(1)} fusion(s32[1024]{0:T(1024)S(1)} %bitcast.90, f32[1024,256]{1,0:T(8,128)} %add_divide_fusion, f32[]{:T(128)} %constant.99.clone.1), kind=kCustom, calls=%fused_computation.78 | custom fusion | flops 262144 | bytes 262656 | tf_op jit(solution)/shard_map/scatter-add | solution.py:57
  133.3 6.6 %scatter_custom_fusion.5 = f32[256,256]{1,0:T(8,128)S(1)} fusion(s32[1024]{0:T(1024)S(1)} %bitcast.88, f32[1024,256]{1,0:T(8,128)} %add_divide_fusion, f32[]{:T(128)} %constant.99.clone.1), kind=kCustom, calls=%fused_computation.76 | custom fusion | flops 262144 | bytes 262656 | tf_op jit(solution)/shard_map/scatter-add | solution.py:58
  140.7 1.1 copy.59
  (69 shorter events, 8.7 us)
Async XLA Ops:
  0.0 8.7 %copy-start.5 = (s32[32]{0:T(128)S(1)}, s32[32]{0:T(128)}, u32[]{:S(2)}) copy-start(s32[32]{0:T(128)} %param.15) | copy-start | bytes 388
  0.0 8.7 %copy-start.6 = (s32[32]{0:T(128)S(1)}, s32[32]{0:T(128)}, u32[]{:S(2)}) copy-start(s32[32]{0:T(128)} %param.14) | copy-start | bytes 388
  0.0 9.0 %copy-start.3 = (s32[1024,2]{0,1:T(2,128)S(1)}, s32[1024,2]{0,1:T(2,128)}, u32[]{:S(2)}) copy-start(s32[1024,2]{0,1:T(2,128)} %param.12) | copy-start | bytes 24580
  1.6 12.3 %copy-start = (f32[64,4,512]{2,1,0:T(4,128)S(1)}, f32[64,4,512]{2,1,0:T(4,128)}, u32[]{:S(2)}) copy-start(f32[64,4,512]{2,1,0:T(4,128)} %param.9) | copy-start | bytes 1572868
  1.6 12.3 %copy-start.1 = (f32[4,512]{1,0:T(4,128)S(1)}, f32[4,512]{1,0:T(4,128)}, u32[]{:S(2)}) copy-start(f32[4,512]{1,0:T(4,128)} %param.10) | copy-start | bytes 24580
  1.7 12.0 %collective-permute-start = (f32[65,2,512]{2,0,1:T(8,128)S(1)}, f32[65,2,512]{2,0,1:T(8,128)S(1)}, u32[]{:S(2)}, u32[]{:S(2)}) collective-permute-start(f32[65,2,512]{2,0,1:T(8,128)S(1)} %copy.43), channel_id=1, source_target_pairs={{1,0},{2,1},{3,2},{4,3},{5,4},{6,5},{7,6},{9,8},{10,9},{11,10},{12... | collective-permute-start | bytes 798728 | tf_op jit(solution)/shard_map/ppermute | solution.py:18
  3.2 17.0 %collective-permute-start.1 = (f32[65,2,512]{2,0,1:T(8,128)S(1)}, f32[65,2,512]{2,0,1:T(8,128)S(1)}, u32[]{:S(2)}, u32[]{:S(2)}) collective-permute-start(f32[65,2,512]{2,0,1:T(8,128)S(1)} %copy.45), channel_id=1, source_target_pairs={{0,1},{1,2},{2,3},{3,4},{4,5},{5,6},{6,7},{8,9},{9,10},{10,11},{11... | collective-permute-start | bytes 798728 | tf_op jit(solution)/shard_map/ppermute | solution.py:15
  22.8 11.6 %collective-permute-start.2 = (f32[65,2,512]{2,0,1:T(8,128)S(1)}, f32[65,2,512]{2,0,1:T(8,128)S(1)}, u32[]{:S(2)}, u32[]{:S(2)}) collective-permute-start(f32[65,2,512]{2,0,1:T(8,128)S(1)} %copy.49), channel_id=1, source_target_pairs={{1,0},{2,1},{3,2},{4,3},{5,4},{6,5},{7,6},{9,8},{10,9},{11,10},{12... | collective-permute-start | bytes 798728 | tf_op jit(solution)/shard_map/ppermute | solution.py:18
  29.0 11.9 %collective-permute-start.3 = (f32[65,2,512]{2,0,1:T(8,128)S(1)}, f32[65,2,512]{2,0,1:T(8,128)S(1)}, u32[]{:S(2)}, u32[]{:S(2)}) collective-permute-start(f32[65,2,512]{2,0,1:T(8,128)S(1)} %copy.51), channel_id=1, source_target_pairs={{0,1},{1,2},{2,3},{3,4},{4,5},{5,6},{6,7},{8,9},{9,10},{10,11},{11... | collective-permute-start | bytes 798728 | tf_op jit(solution)/shard_map/ppermute | solution.py:15
  43.3 4.5 %copy-start.4 = (s32[1024,2]{0,1:T(2,128)S(1)}, s32[1024,2]{0,1:T(2,128)}, u32[]{:S(2)}) copy-start(s32[1024,2]{0,1:T(2,128)} %param.13) | copy-start | bytes 24580
  44.2 12.3 %all-to-all-start = ((f32[4,64,4,128]{3,2,1,0:T(4,128)}), f32[4,64,4,128]{3,2,1,0:T(4,128)S(1)}, u32[]{:S(2)}, u32[]{:S(2)}) async-start(f32[4,64,4,128]{3,2,1,0:T(4,128)} %pad_maximum_fusion.7), calls=%async_computation | async-start | bytes 1048576 | tf_op jit(solution)/shard_map/all_to_all | solution.py:76
  56.6 7.6 %collective-permute-start.5 = (f32[256,1,128]{2,0,1:T(8,128)S(1)}, f32[256,1,128]{2,0,1:T(8,128)S(1)}, u32[]{:S(2)}, u32[]{:S(2)}) collective-permute-start(f32[256,1,128]{2,0,1:T(8,128)S(1)} %get-tuple-element.23), channel_id=1, source_target_pairs={{1,0},{2,1},{3,2},{4,3},{5,4},{6,5},{7,6},{9,8},{10,9},{11,10},{12... | collective-permute-start | bytes 393224 | tf_op jit(solution)/shard_map/ppermute | solution.py:26
  57.9 9.7 %collective-permute-start.4 = (f32[256,1,128]{2,0,1:T(8,128)S(1)}, f32[256,1,128]{2,0,1:T(8,128)S(1)}, u32[]{:S(2)}, u32[]{:S(2)}) collective-permute-start(f32[256,1,128]{2,0,1:T(8,128)S(1)} %get-tuple-element.22), channel_id=1, source_target_pairs={{0,1},{1,2},{2,3},{3,4},{4,5},{5,6},{6,7},{8,9},{9,10},{10,11},{11... | collective-permute-start | bytes 393224 | tf_op jit(solution)/shard_map/ppermute | solution.py:26
  72.7 3.5 %copy-start.2 = (f32[1024]{0:T(1024)S(1)}, f32[1024]{0:T(1024)}, u32[]{:S(2)}) copy-start(f32[1024]{0:T(1024)} %param.11) | copy-start | bytes 12292
